TPU v7x, 256 devices: a whole 4x4x8 slice. The times are simulated.
256 devices in a mesh: gp: 256 (over z, y, x, core).
Axes of the slice: x: 4, y: 4, z: 8, core: 2. Of those that a mesh axis runs over, the one named last changes fastest.
Arguments:
- features: bfloat16 [524288, 100], P('gp')
- labels: int32 [524288], P('gp')
- train_mask: float32 [524288], P('gp')
- send_idx: int32 [65536, 8], P('gp')
- src_idx: int32 [4194304], P('gp')
- dst_idx: int32 [4194304], P('gp')
- inv_deg: float32 [524288], P('gp')
- w_self_1: bfloat16 [100, 256], replicated
- w_neigh_1: bfloat16 [100, 256], replicated
- bias_1: float32 [256], replicated
- w_self_2: bfloat16 [256, 256], replicated
- w_neigh_2: bfloat16 [256, 256], replicated
- bias_2: float32 [256], replicated
- w_self_3: bfloat16 [256, 47], replicated
- w_neigh_3: bfloat16 [256, 47], replicated
- bias_3: float32 [47], replicated
Outputs:
- output 1: float32 [], replicated
- output 2: float32 [100, 256], replicated
- output 3: float32 [100, 256], replicated
- output 4: float32 [256], replicated
- output 5: float32 [256, 256], replicated
- output 6: float32 [256, 256], replicated
- output 7: float32 [256], replicated
- output 8: float32 [256, 47], replicated
- output 9: float32 [256, 47], replicated
- output 10: float32 [47], replicated
All inputs are finite; a program needn't handle non-finite values.
Results may differ from a plain program's by a relative error of at most 0.0069051.
Values are sent between devices in bfloat16 or wider.
A program may use at most 768 MiB of HBM per device.

v0:
```python
import jax
import jax.numpy as jnp
from jax import lax
from jax.sharding import PartitionSpec as P

GROUP_AXIS = 'gp'


def aggregate(table, src_idx, dst_idx, inv_deg):
    gathered = jnp.take(table, src_idx, axis=0).astype(jnp.float32)
    summed = jax.ops.segment_sum(gathered, dst_idx, num_segments=inv_deg.shape[0], indices_are_sorted=True)
    return (summed * inv_deg[:, None]).astype(jnp.bfloat16)


def aggregate_grad(d_mean, src_idx, dst_idx, inv_deg, table_rows):
    d_sum = d_mean * inv_deg[:, None]
    return jax.ops.segment_sum(jnp.take(d_sum, dst_idx, axis=0), src_idx, num_segments=table_rows)


def weight_grads(h_in, neigh_mean, d_pre, d_pre_bf):
    g_self = jnp.einsum('nd,ne->de', h_in, d_pre_bf, preferred_element_type=jnp.float32)
    g_neigh = jnp.einsum('nd,ne->de', neigh_mean, d_pre_bf, preferred_element_type=jnp.float32)
    return g_self, g_neigh, jnp.sum(d_pre, axis=0)


def input_grads(d_pre_bf, w_self, w_neigh):
    d_self = jnp.einsum('ne,de->nd', d_pre_bf, w_self, preferred_element_type=jnp.float32)
    d_mean = jnp.einsum('ne,de->nd', d_pre_bf, w_neigh, preferred_element_type=jnp.float32)
    return d_self, d_mean


def head_grad(logits, labels, train_mask):
    log_prob = jax.nn.log_softmax(logits, axis=-1)
    is_label = labels[:, None] == jnp.arange(logits.shape[1], dtype=jnp.int32)[None, :]
    picked = jnp.sum(jnp.where(is_label, log_prob, 0.0), axis=-1)
    d_logits = (jnp.exp(log_prob) - is_label.astype(jnp.float32)) * train_mask[:, None]
    return jnp.sum(train_mask * -picked), d_logits


def solution(mesh):
    def device_step(features, labels, train_mask, send_idx, src_idx, dst_idx, inv_deg,
                    w_self_1, w_neigh_1, bias_1, w_self_2, w_neigh_2, bias_2,
                    w_self_3, w_neigh_3, bias_3):
        n_own = features.shape[0]
        send_flat = send_idx.reshape(-1)
        table_rows = n_own + send_flat.shape[0]

        def layer(hidden, w_self, w_neigh, bias):
            outgoing = jnp.take(hidden, send_flat, axis=0)
            received = lax.all_to_all(outgoing, GROUP_AXIS, 0, 0, tiled=True)
            table = jnp.concatenate([hidden, received], axis=0)
            neigh_mean = aggregate(table, src_idx, dst_idx, inv_deg)
            pre_act = (jnp.dot(hidden, w_self, preferred_element_type=jnp.float32)
                       + jnp.dot(neigh_mean, w_neigh, preferred_element_type=jnp.float32) + bias)
            return neigh_mean, pre_act

        def back_to_owners(d_mean):
            d_table = aggregate_grad(d_mean, src_idx, dst_idx, inv_deg, table_rows)
            returned = lax.all_to_all(d_table[n_own:].astype(jnp.bfloat16), GROUP_AXIS, 0, 0, tiled=True)
            owner_sum = jax.ops.segment_sum(returned.astype(jnp.float32), send_flat, num_segments=n_own)
            return d_table[:n_own] + owner_sum

        mean_1, pre_1 = layer(features, w_self_1, w_neigh_1, bias_1)
        hidden_1 = jax.nn.relu(pre_1).astype(jnp.bfloat16)
        mean_2, pre_2 = layer(hidden_1, w_self_2, w_neigh_2, bias_2)
        hidden_2 = jax.nn.relu(pre_2).astype(jnp.bfloat16)
        mean_3, logits = layer(hidden_2, w_self_3, w_neigh_3, bias_3)
        loss_sum, d_logits = head_grad(logits, labels, train_mask)
        totals = lax.psum(jnp.stack([loss_sum, jnp.sum(train_mask)]), GROUP_AXIS)

        d_pre_3 = d_logits / totals[1]
        d_bf_3 = d_pre_3.astype(jnp.bfloat16)
        g_self_3, g_neigh_3, g_bias_3 = weight_grads(hidden_2, mean_3, d_pre_3, d_bf_3)
        d_self_3, d_mean_3 = input_grads(d_bf_3, w_self_3, w_neigh_3)
        d_pre_2 = jnp.where(pre_2 > 0, d_self_3 + back_to_owners(d_mean_3), 0.0)
        d_bf_2 = d_pre_2.astype(jnp.bfloat16)
        g_self_2, g_neigh_2, g_bias_2 = weight_grads(hidden_1, mean_2, d_pre_2, d_bf_2)
        d_self_2, d_mean_2 = input_grads(d_bf_2, w_self_2, w_neigh_2)
        d_pre_1 = jnp.where(pre_1 > 0, d_self_2 + back_to_owners(d_mean_2), 0.0)
        d_bf_1 = d_pre_1.astype(jnp.bfloat16)
        g_self_1, g_neigh_1, g_bias_1 = weight_grads(features, mean_1, d_pre_1, d_bf_1)

        grads = lax.psum((g_self_1, g_neigh_1, g_bias_1, g_self_2, g_neigh_2, g_bias_2,
                          g_self_3, g_neigh_3, g_bias_3), GROUP_AXIS)
        return (totals[0] / totals[1],) + tuple(grads)

    sharded = P(GROUP_AXIS)
    whole = P()
    return jax.shard_map(device_step, mesh=mesh,
                         in_specs=(sharded,) * 7 + (whole,) * 9,
                         out_specs=(whole,) * 10, check_vma=False)
```

profile of v0, /device:TPU:1, one launch (start us, length us, event | category | flops | bytes accessed | tf_op | source)
XLA Modules:
  0.0 1837.2 jit_solution(17114232293726003809)
XLA Ops:
  7.9 0.8 copy.30
  9.1 1.3 copy.32
  10.4 6.2 gather_fusion
  16.6 1.1 bitcast_select_fusion
  17.7 15.7 all-to-all-start
  33.6 19.1 %all-to-all-done = bf16[256,8,100]{2,1,0:T(8,128)(2,1)S(1)} async-done(((bf16[256,8,100]{2,1,0:T(8,128)(2,1)}), bf16[256,8,100]{2,1,0:T(8,128)(2,1)S(1)}, u32[]{:S(2)}, u32[]{:S(2)}) %all-to-all-start) | async-done | bytes 409632 | tf_op jit(solution)/shard_map/all_to_all | solution.py:50
  52.9 162.7 %scatter_custom_fusion = f32[2048,100]{1,0:T(8,128)S(1)} fusion(s32[16384]{0:T(1024)} %param.27, pred[16384]{0:T(1024)(128)(4,1)S(1)} %compare_and_fusion.1, bf16[]{:T(256)} %constant.63.clone.1, f32[]{:T(128)} %constant.54.clone.1, bf16[4096,100]{1,0:T(8,128)(2,1)S(1)} %pad_maximum_fusion.2, s32[16384]{0:T(1024)S(1)} %fusion.43), kind=kCustom, calls=%fused_computation.27 | custom fusion | flops 4915200 | bytes 1721344 | tf_op jit(solution)/shard_map/scatter-add | solution.py:11
  215.6 1.0 copy-done.6
  217.6 1.8 maximum_convert_fusion.1
  219.4 7.5 gather_fusion.1
  226.9 1.2 select_bitcast_fusion.1
  228.2 7.1 all-to-all-start.1
  235.3 1.7 fusion.59
  237.0 28.2 %all-to-all-done.1 = bf16[256,8,256]{2,1,0:T(8,128)(2,1)S(1)} async-done(((bf16[256,8,256]{2,1,0:T(8,128)(2,1)}), bf16[256,8,256]{2,1,0:T(8,128)(2,1)S(1)}, u32[]{:S(2)}, u32[]{:S(2)}) %all-to-all-start.1) | async-done | bytes 1048608 | tf_op jit(solution)/shard_map/all_to_all | solution.py:50
  265.2 1.0 copy-done.8
  266.2 1.4 pad_maximum_fusion
  267.6 166.0 %scatter_custom_fusion.1 = f32[2048,256]{1,0:T(8,128)} fusion(s32[16384]{0:T(1024)S(1)} %copy-done.17, pred[16384]{0:T(1024)(128)(4,1)S(1)} %compare_and_fusion.1, bf16[]{:T(256)} %constant.63.clone.1, f32[]{:T(128)} %constant.54.clone.1, bf16[4096,256]{1,0:T(8,128)(2,1)S(1)} %pad_maximum_fusion, s32[16384]{0:T(1024)S(1)} %fusion.43), kind=kCustom, calls=%fused_computation.21 | custom fusion | flops 12582912 | bytes 4276230 | tf_op jit(solution)/shard_map/scatter-add | solution.py:11
  433.6 4.1 maximum_convert_fusion
  437.7 7.5 gather_fusion.2
  445.2 1.3 select_bitcast_fusion
  446.5 6.7 all-to-all-start.2
  453.3 1.2 fusion.60
  454.5 28.8 %all-to-all-done.2 = bf16[256,8,256]{2,1,0:T(8,128)(2,1)S(1)} async-done(((bf16[256,8,256]{2,1,0:T(8,128)(2,1)}), bf16[256,8,256]{2,1,0:T(8,128)(2,1)S(1)}, u32[]{:S(2)}, u32[]{:S(2)}) %all-to-all-start.2) | async-done | bytes 1048608 | tf_op jit(solution)/shard_map/all_to_all | solution.py:50
  483.3 1.5 pad_maximum_fusion.1
  484.8 216.5 %scatter_custom_fusion.2 = f32[2048,256]{1,0:T(8,128)} fusion(s32[16384]{0:T(1024)S(1)} %copy-done.17, pred[16384]{0:T(1024)(128)(4,1)S(1)} %copy-done.16, bf16[]{:T(256)} %constant.63.clone.1, f32[]{:T(128)} %constant.54.clone.1, bf16[4096,256]{1,0:T(8,128)(2,1)} %pad_maximum_fusion.1, s32[16384]{0:T(1024)S(1)} %fusion.43), kind=kCustom, calls=%fused_computation.19 | custom fusion | flops 12582912 | bytes 4276230 | tf_op jit(solution)/shard_map/scatter-add | solution.py:11
  701.3 2.1 fusion.58
  704.3 1.4 pad_maximum_fusion.3
  705.7 74.8 %psum.70 = f32[2]{0:T(128)S(1)} all-reduce(f32[2]{0:T(128)S(1)} %pad_maximum_fusion.3), channel_id=1, replica_groups=mesh['gp'=256] {'gp'}, use_global_device_ids=true, to_apply=%region_8.11 | all-reduce | flops 2 | bytes 16 | tf_op jit(solution)/shard_map/psum | solution.py:69
  781.0 1.5 fusion.46
  782.5 1.8 convolution_multiply_fusion
  784.3 189.0 %scatter_custom_fusion.3 = f32[4096,256]{1,0:T(8,128)} fusion(s32[16384]{0:T(1024)} %param.26, f32[]{:T(128)} %constant.47.clone.2, pred[16384]{0:T(1024)(128)(4,1)S(1)} %compare_and_fusion, f32[]{:T(128)} %constant.54.clone.1, f32[2048,256]{1,0:T(8,128)} %convolution_multiply_fusion, s32[16384]{0:T(1024)S(1)} %fusion.44), kind=kCustom, calls=%fused_computation.17 | custom fusion | flops 8388608 | bytes 6374400 | tf_op jit(solution)/shard_map/scatter-add | solution.py:17
  973.4 2.7 fusion.32
  976.0 6.6 all-to-all-start.3
  982.7 3.4 convolution_add_fusion
  986.1 26.6 %all-to-all-done.3 = bf16[256,8,256]{2,1,0:T(8,128)(2,1)S(1)} async-done(((bf16[256,8,256]{2,1,0:T(8,128)(2,1)}), bf16[256,8,256]{2,1,0:T(8,128)(2,1)S(1)}, u32[]{:S(2)}, u32[]{:S(2)}) %all-to-all-start.3) | async-done | bytes 1048608 | tf_op jit(solution)/shard_map/all_to_all | solution.py:59
  1012.7 14.7 scatter_custom_fusion.4
  1027.4 2.5 fusion.41
  1029.9 1.8 convolution_multiply_fusion.1
  1031.8 196.7 %scatter_custom_fusion.5 = f32[4096,256]{1,0:T(8,128)} fusion(s32[16384]{0:T(1024)} %param.26, f32[]{:T(128)} %constant.47.clone.2, pred[16384]{0:T(1024)(128)(4,1)} %copy-done.19, f32[]{:T(128)} %constant.54.clone.1, f32[2048,256]{1,0:T(8,128)} %convolution_multiply_fusion.1, s32[16384]{0:T(1024)S(1)} %fusion.44), kind=kCustom, calls=%fused_computation.15 | custom fusion | flops 8388608 | bytes 6374400 | tf_op jit(solution)/shard_map/scatter-add | solution.py:17
  1228.5 2.7 fusion.33
  1231.2 8.3 all-to-all-start.4
  1239.8 0.9 fusion.62
  1240.7 2.7 fusion.56
  1243.4 2.6 fusion.40
  1246.0 1.2 fusion.61
  1247.7 1.5 fusion.55
  1249.2 1.8 convolution_add_fusion.2
  1251.1 17.6 all-to-all-done.4
  1268.6 14.9 scatter_custom_fusion.6
  1283.5 2.6 fusion.38
  1286.6 0.8 copy-done.7
  1287.4 1.3 fusion.53
  1288.8 0.9 convolution_bitcast_fusion
  1291.1 255.3 %all-reduce.5.cloned.1.call-done = (f32[256]{0:T(256)}, f32[256]{0:T(256)}, f32[256,47]{0,1:T(8,128)}, f32[256,47]{0,1:T(8,128)}, f32[47]{0:T(128)}) async-done(((f32[256]{0:T(256)}, f32[256]{0:T(256)}, f32[256,47]{0,1:T(8,128)}, f32[256,47]{0,1:T(8,128)}, f32[47]{0:T(128)}), (f32[256]{0:T(256)}, f32[256]{0:T(256)}, f32[256,47]{0,1:T(8,128)}, f32[256,47]{0,1:T(8,128)}, ...) | async-done | bytes 98508 | tf_op jit(solution)/shard_map/psum | solution.py:83
  1546.3 269.8 %all-reduce.7.cloned.1.call-done = (f32[100,256]{1,0:T(8,128)}, f32[100,256]{1,0:T(8,128)}, f32[256,256]{1,0:T(8,128)}, f32[256,256]{1,0:T(8,128)}) async-done(((f32[100,256]{1,0:T(8,128)}, f32[100,256]{1,0:T(8,128)}, f32[256,256]{1,0:T(8,128)}, f32[256,256]{1,0:T(8,128)}), (f32[100,256]{1,0:T(8,128)}, f32[100,256]{1,0:T(8,128)}, f32[256,256]{1,0:T(8,128)}, ...) | async-done | bytes 729104 | tf_op jit(solution)/shard_map/psum | solution.py:83
  1816.1 1.5 copy.45
  1817.7 1.5 copy.46
  1819.2 1.2 copy.47
  1820.5 1.7 copy.48
  1822.1 1.7 copy.49
  1823.8 1.2 copy.50
  1825.0 1.4 copy.51
  1826.4 1.4 copy.52
  1827.9 1.1 copy.53
  (79 shorter events, 5.2 us)
Async XLA Ops:
  7.2 426.5 %copy-start = (bf16[256,256]{1,0:T(8,128)(2,1)S(1)}, bf16[256,256]{1,0:T(8,128)(2,1)}, u32[]{:S(2)}) copy-start(bf16[256,256]{1,0:T(8,128)(2,1)} %param.33) | copy-start | bytes 393220
  16.6 16.9 copy-start.18
  17.7 35.0 %all-to-all-start = ((bf16[256,8,100]{2,1,0:T(8,128)(2,1)}), bf16[256,8,100]{2,1,0:T(8,128)(2,1)S(1)}, u32[]{:S(2)}, u32[]{:S(2)}) async-start(bf16[256,8,100]{2,1,0:T(8,128)(2,1)} %bitcast_select_fusion), calls=%async_computation | async-start | bytes 1048576 | tf_op jit(solution)/shard_map/all_to_all | solution.py:50
  33.5 234.0 %copy-start.15 = (pred[16384]{0:T(1024)(128)(4,1)}, pred[16384]{0:T(1024)(128)(4,1)S(1)}, u32[]{:S(2)}) copy-start(pred[16384]{0:T(1024)(128)(4,1)S(1)} %compare_and_fusion.1) | copy-start | bytes 49156
  52.7 163.9 %copy-start.12 = (f32[2048]{0:T(1024)S(1)}, f32[2048]{0:T(1024)}, u32[]{:S(2)}) copy-start(f32[2048]{0:T(1024)} %param.28) | copy-start | bytes 24580
  52.7 163.9 %copy-start.22 = (bf16[100,256]{1,0:T(8,128)(2,1)S(1)}, bf16[100,256]{1,0:T(8,128)(2,1)}, u32[]{:S(2)}) copy-start(bf16[100,256]{1,0:T(8,128)(2,1)} %param.30) | copy-start | bytes 153604
  215.6 1.0 copy-start.6
  216.6 1.0 copy-start.9
  216.6 1.0 copy-start.23
  216.6 1.0 copy-start.27
  226.9 8.4 copy-start.13
  228.2 37.0 %all-to-all-start.1 = ((bf16[256,8,256]{2,1,0:T(8,128)(2,1)}), bf16[256,8,256]{2,1,0:T(8,128)(2,1)S(1)}, u32[]{:S(2)}, u32[]{:S(2)}) async-start(bf16[256,8,256]{2,1,0:T(8,128)(2,1)} %select_bitcast_fusion.1), calls=%async_computation.1 | async-start | bytes 2097152 | tf_op jit(solution)/shard_map/all_to_all | solution.py:50
  265.2 1.0 copy-start.8
  266.2 1.4 copy-start.17
  267.6 166.0 %copy-start.26 = (f32[256]{0:T(256)S(1)}, f32[256]{0:T(256)}, u32[]{:S(2)}) copy-start(f32[256]{0:T(256)} %param.34) | copy-start | bytes 3076
  445.2 8.1 copy-start.21
  446.5 36.8 %all-to-all-start.2 = ((bf16[256,8,256]{2,1,0:T(8,128)(2,1)}), bf16[256,8,256]{2,1,0:T(8,128)(2,1)S(1)}, u32[]{:S(2)}, u32[]{:S(2)}) async-start(bf16[256,8,256]{2,1,0:T(8,128)(2,1)} %select_bitcast_fusion), calls=%async_computation.2 | async-start | bytes 2097152 | tf_op jit(solution)/shard_map/all_to_all | solution.py:50
  483.3 1.5 copy-start.16
  484.8 216.5 %copy-start.11 = (f32[2048,47]{0,1:T(8,128)S(1)}, f32[2048,47]{0,1:T(8,128)}, u32[]{:S(2)}) copy-start(f32[2048,47]{0,1:T(8,128)} %fusion.60) | copy-start | bytes 1155076
  484.8 216.5 %copy-start.20 = (bf16[256,47]{0,1:T(8,128)(2,1)S(1)}, bf16[256,47]{0,1:T(8,128)(2,1)}, u32[]{:S(2)}) copy-start(bf16[256,47]{0,1:T(8,128)(2,1)} %param.36) | copy-start | bytes 72196
  484.8 216.5 %copy-start.28 = (f32[47]{0:T(128)S(1)}, f32[47]{0:T(128)}, u32[]{:S(2)}) copy-start(f32[47]{0:T(128)} %param.37) | copy-start | bytes 568
  701.3 2.2 copy-start.25
  701.3 2.3 copy-start.24
  705.7 267.7 %copy-start.19 = (pred[16384]{0:T(1024)(128)(4,1)}, pred[16384]{0:T(1024)(128)(4,1)S(1)}, u32[]{:S(2)}) copy-start(pred[16384]{0:T(1024)(128)(4,1)S(1)} %compare_and_fusion) | copy-start | bytes 49156
  976.0 36.7 %all-to-all-start.3 = ((bf16[256,8,256]{2,1,0:T(8,128)(2,1)}), bf16[256,8,256]{2,1,0:T(8,128)(2,1)S(1)}, u32[]{:S(2)}, u32[]{:S(2)}) async-start(bf16[256,8,256]{2,1,0:T(8,128)(2,1)} %fusion.32), calls=%async_computation.3 | async-start | bytes 2097152 | tf_op jit(solution)/shard_map/all_to_all | solution.py:59
  1231.2 37.5 %all-to-all-start.4 = ((bf16[256,8,256]{2,1,0:T(8,128)(2,1)}), bf16[256,8,256]{2,1,0:T(8,128)(2,1)}, u32[]{:S(2)}, u32[]{:S(2)}) async-start(bf16[256,8,256]{2,1,0:T(8,128)(2,1)} %fusion.33), calls=%async_computation.4 | async-start | bytes 2097152 | tf_op jit(solution)/shard_map/all_to_all | solution.py:59
  1239.4 306.9 %all-reduce.5.cloned.1.call-start = ((), (), s32[]{:S(2)}) async-start(), calls=%async_computation.5 | async-start | bytes 201728 | tf_op jit(solution)/shard_map/psum | solution.py:83
  1239.7 3.6 copy-start.2
  1243.4 5.9 copy-start.5
  1246.0 1.7 copy-start.1
  1247.7 1.6 copy-start.14
  1251.1 32.5 %copy-start.3 = (f32[2048,256]{1,0:T(8,128)S(1)}, f32[2048,256]{1,0:T(8,128)}, u32[]{:S(2)}) copy-start(f32[2048,256]{1,0:T(8,128)} %get-tuple-element.29) | copy-start | bytes 6291460
  1283.5 2.6 copy-start.4
  1286.1 1.2 copy-start.7
  1287.4 1.4 copy-start.10
  1288.7 527.4 %all-reduce.7.cloned.1.call-start = ((), (), s32[]{:S(2)}) async-start(), calls=%async_computation.6 | async-start | bytes 1474560 | tf_op jit(solution)/shard_map/psum | solution.py:83
Sparse Core Ops, SparseCore 0:
  1288.8 257.4 all-reduce.4
  1552.9 263.1 all-reduce.6
where the time goes:
time: 1850 us; the launch traced here: 1840 us
  other arithmetic  980 us (53%)
  waiting for transfers between devices  645 us (35%)
  blocking collectives  74.8 us (4%)
  local copies, waits for them, and re-layouts  46.3 us (3%)
  starting transfers between devices  44.7 us (2%)
  matrix products  28.9 us (2%)
    scatter-add x3, other arithmetic, aggregate(): jax.ops.segment_sum(gathered, dst_idx, num_segments=inv_deg.shape[0], ind...  545 us
    psum x2, waiting for transfers between devices, device_step(): lax.psum((g_self_1, g_neigh_1, g_bias_1, g_self_2, g_neigh_2, g_bias_2, g...  525 us
    scatter-add x2, other arithmetic, aggregate_grad(): jax.ops.segment_sum(jnp.take(d_sum, dst_idx, axis=0), src_idx, num_segmen...  386 us
    all_to_all x3, waiting for transfers between devices, layer(): received = lax.all_to_all(outgoing, GROUP_AXIS, 0, 0, tiled=True)  76.1 us
    psum x1, blocking collectives, device_step(): totals = lax.psum(jnp.stack([loss_sum, jnp.sum(train_mask)]), GROUP_AXIS)  74.8 us
    all_to_all x2, waiting for transfers between devices, back_to_owners(): lax.all_to_all(d_table[n_own:].astype(jnp.bfloat16), GROUP_AXIS, 0, 0, ti...  44.2 us
  transfers between devices with their start and end apart: 7, of which 7 were waited for; matrix products, arithmetic and copies ran while one was open for 1% of the time, Pallas kernels for 0%

commit v1 on v0

v1 whole, which is shorter than its diff:
```python
import functools

import jax
import jax.numpy as jnp
from jax import lax
from jax.experimental import pallas as pl
from jax.experimental.pallas import tpu as pltpu
from jax.sharding import PartitionSpec as P

AXIS = 'gp'
BF = jnp.bfloat16
F32 = jnp.float32
TILE = 256
LANES = 128
DST_TILE = 16
SRC_LO = 256
MAX_EXACT = 256
EXTRA = 128
CLS = 48

VMEM = pl.BlockSpec(memory_space=pltpu.VMEM)
SMEM = pl.BlockSpec(memory_space=pltpu.SMEM)
ANY = pl.BlockSpec(memory_space=pl.ANY)
VMEM_LIMIT = 63 * 1024 * 1024


def dot(a, b):
    return lax.dot_general(a, b, (((1,), (0,)), ((), ())), preferred_element_type=F32)


def dot_t(a, b):
    return lax.dot_general(a, b, (((1,), (1,)), ((), ())), preferred_element_type=F32)


def onehot(mask):
    return jnp.where(mask, 1.0, 0.0).astype(BF)


def rows_at(t, size=TILE):
    return pl.ds(pl.multiple_of(t * size, size), size)


def identity(size=TILE):
    return onehot(lax.broadcasted_iota(jnp.int32, (size, size), 0)
                  == lax.broadcasted_iota(jnp.int32, (size, size), 1))


def build_kernel(starts, dst_ref, src_ref, a_ref, extra_ref, pick_ref, acc_ref, count_ref):
    step = pl.program_id(0)
    tiles = a_ref.shape[0] // DST_TILE
    n_hi = a_ref.shape[1] // SRC_LO
    chunk_rows = SRC_LO // LANES

    @pl.when(step == 0)
    def _():
        pick_ref[...] = jnp.zeros_like(pick_ref)
        count_ref[0] = 0

    extra_ref[...] = jnp.zeros_like(extra_ref)

    def partial(tile, row):
        iota = lax.broadcasted_iota(jnp.int32, (n_hi * DST_TILE, LANES), 0)
        iota_lo = lax.broadcasted_iota(jnp.int32, (SRC_LO, LANES), 0)
        left, right = [], []
        for k in range(chunk_rows):
            src = src_ref[row + k]
            local = dst_ref[row + k] - tile * DST_TILE
            inside = (local >= 0) & (local < DST_TILE)
            code = jnp.where(inside, lax.shift_right_logical(src, 8) * DST_TILE + local, -1)
            left.append(onehot(iota == code))
            right.append(onehot(iota_lo == (src & (SRC_LO - 1))))
        return dot_t(jnp.concatenate(left, axis=1), jnp.concatenate(right, axis=1))

    def store(u, acc):
        out = acc.astype(BF)
        for hi in range(n_hi):
            a_ref[pl.ds(pl.multiple_of(u * DST_TILE, DST_TILE), DST_TILE), hi * SRC_LO:(hi + 1) * SRC_LO] = (
                out[hi * DST_TILE:(hi + 1) * DST_TILE])

    def one(u):
        tile = step * tiles + u
        store(u, partial(tile, starts[tile] // LANES))

    def many(u):
        tile = step * tiles + u
        first = starts[tile] // LANES
        last = starts[tile + 1]
        n_chunks = (last - first * LANES + SRC_LO - 1) // SRC_LO

        @pl.when(n_chunks > 1)
        def _():
            acc_ref[...] = jnp.zeros_like(acc_ref)

            def add(c, _):
                acc_ref[...] += partial(tile, first + c * chunk_rows)
                return 0

            lax.fori_loop(0, n_chunks, add, 0)
            store(u, acc_ref[...])

            @pl.when(last - starts[tile] > MAX_EXACT)
            def _():
                acc_ref[...] -= acc_ref[...].astype(BF).astype(F32)
                flat = (lax.broadcasted_iota(jnp.int32, acc_ref.shape, 0) * SRC_LO
                        + lax.broadcasted_iota(jnp.int32, acc_ref.shape, 1))

                def left():
                    return jnp.max(jnp.where(acc_ref[...] != 0.0, flat, -1))

                def move(at):
                    value = jnp.sum(jnp.where(flat == at, acc_ref[...], 0.0))
                    code, lo = at // SRC_LO, at % SRC_LO
                    hi, local = code // DST_TILE, code % DST_TILE
                    k = count_ref[0]
                    here = pl.ds(pl.multiple_of(u * DST_TILE, DST_TILE), DST_TILE)
                    shape = (DST_TILE, EXTRA)
                    hit = ((lax.broadcasted_iota(jnp.int32, shape, 0) == local)
                           & (lax.broadcasted_iota(jnp.int32, shape, 1) == k))
                    extra_ref[here, :] = jnp.where(hit, value, extra_ref[here, :].astype(F32)).astype(BF)
                    group = pl.ds(pl.multiple_of(k // DST_TILE * DST_TILE, DST_TILE), DST_TILE)
                    shape = (DST_TILE, pick_ref.shape[1])
                    hit = ((lax.broadcasted_iota(jnp.int32, shape, 0) == k % DST_TILE)
                           & (lax.broadcasted_iota(jnp.int32, shape, 1) == hi * SRC_LO + lo))
                    pick_ref[group, :] = jnp.where(hit, 1.0, pick_ref[group, :].astype(F32)).astype(BF)
                    count_ref[0] = k + 1
                    acc_ref[...] = jnp.where(flat == at, 0.0, acc_ref[...])
                    return left()

                lax.while_loop(lambda at: at >= 0, move, left())

    unroll = 4

    def group(g, _):
        for k in range(unroll):
            one(g * unroll + k)
        for k in range(unroll):
            many(g * unroll + k)
        return 0

    lax.fori_loop(0, tiles // unroll, group, 0)


def build_adjacency(dst_idx, src_idx, n_own, table_rows):
    edges = dst_idx.shape[0]
    tiles = n_own // DST_TILE
    bounds = jnp.arange(tiles + 1, dtype=jnp.int32) * DST_TILE
    starts = jnp.sum((dst_idx[None, :] < bounds[:, None]).astype(jnp.int32), axis=1)
    rows = edges // LANES
    pad = SRC_LO // LANES
    dst3 = jnp.pad(dst_idx.reshape(rows, 1, LANES), ((0, pad), (0, 0), (0, 0)), constant_values=-1)
    src3 = jnp.pad(src_idx.reshape(rows, 1, LANES), ((0, pad), (0, 0), (0, 0)))
    block = n_own // 8
    return pl.pallas_call(
        build_kernel,
        grid_spec=pltpu.PrefetchScalarGridSpec(
            num_scalar_prefetch=1,
            grid=(n_own // block,),
            in_specs=[pl.BlockSpec(dst3.shape, lambda i, s: (0, 0, 0)),
                      pl.BlockSpec(src3.shape, lambda i, s: (0, 0, 0))],
            out_specs=[pl.BlockSpec((block, table_rows), lambda i, s: (i, 0)),
                       pl.BlockSpec((block, EXTRA), lambda i, s: (i, 0)),
                       pl.BlockSpec((EXTRA, table_rows), lambda i, s: (0, 0))],
            scratch_shapes=[pltpu.VMEM((table_rows // SRC_LO * DST_TILE, SRC_LO), F32),
                            pltpu.SMEM((1,), jnp.int32)]),
        out_shape=[jax.ShapeDtypeStruct((n_own, table_rows), BF),
                   jax.ShapeDtypeStruct((n_own, EXTRA), BF),
                   jax.ShapeDtypeStruct((EXTRA, table_rows), BF)],
        compiler_params=pltpu.CompilerParams(vmem_limit_bytes=24 * 1024 * 1024),
        cost_estimate=pl.CostEstimate(flops=2 * edges * 2 * SRC_LO * SRC_LO, bytes_accessed=2 * n_own * table_rows,
                                      transcendentals=0),
        name='build_adjacency',
    )(starts, dst3, src3)


def load_adjacency(a_hbm, a_ref, sems):
    blocks = sems.shape[0]
    size = a_ref.shape[0] // blocks
    copies = [pltpu.make_async_copy(a_hbm.at[pl.ds(b * size, size)], a_ref.at[pl.ds(b * size, size)], sems.at[b])
              for b in range(blocks)]
    for copy in copies:
        copy.start()
    return copies


def send_rows(hidden_ref, send_col_ref, out_ref):
    n_own = hidden_ref.shape[0]

    def one(t, _):
        wanted = jnp.concatenate([send_col_ref[rows_at(t)]] * (n_own // LANES), axis=1)
        pick = onehot(wanted == lax.broadcasted_iota(jnp.int32, (TILE, n_own), 1))
        out_ref[rows_at(t)] = dot(pick, hidden_ref[...]).astype(BF)
        return 0

    lax.fori_loop(0, out_ref.shape[0] // TILE, one, 0)


def owner_sums(send_row_ref, returned_ref, t):
    n_recv = returned_ref.shape[0]
    owned = lax.broadcasted_iota(jnp.int32, (TILE, n_recv), 0) + t * TILE
    return dot(onehot(owned == send_row_ref[...]), returned_ref[...])


def aggregate(a_ref, extra_ref, table_ref, picked, inv_ref, t):
    width = table_ref.shape[1]
    total = dot(a_ref[rows_at(t)], table_ref[...]) + dot(extra_ref[rows_at(t)], picked)
    inv = inv_ref[rows_at(t)]
    if width > LANES:
        inv = jnp.concatenate([inv] * (width // LANES), axis=1)
    return (total * inv).astype(BF)


def layer_kernel(own_ref, recv_ref, a_hbm, extra_ref, pick_ref, inv_ref, send_col_ref, w_self_ref, w_neigh_ref, bias_ref,
                 h_ref, mean_ref, out_ref, a_ref, table_ref, sems):
    n_own = own_ref.shape[0]
    copies = load_adjacency(a_hbm, a_ref, sems)
    table_ref[:n_own] = own_ref[...]
    table_ref[n_own:] = recv_ref[...]
    picked = dot(pick_ref[...], table_ref[...]).astype(BF)
    for copy in copies:
        copy.wait()

    def one(t, _):
        mean = aggregate(a_ref, extra_ref, table_ref, picked, inv_ref, t)
        mean_ref[rows_at(t)] = mean
        pre = dot(own_ref[rows_at(t)], w_self_ref[...]) + dot(mean, w_neigh_ref[...]) + bias_ref[...]
        h_ref[rows_at(t)] = jnp.maximum(pre, 0.0).astype(BF)
        return 0

    lax.fori_loop(0, n_own // TILE, one, 0)
    send_rows(h_ref, send_col_ref, out_ref)


def gather_kernel(own_ref, send_col_ref, out_ref):
    send_rows(own_ref, send_col_ref, out_ref)


def column_product(left, a_ref, extra_ref, pick_ref, t):
    at = rows_at(t)
    total = dot(left, a_ref[:, at])
    rest = dot(left, extra_ref[...])
    high = rest.astype(BF)
    low = (rest - high.astype(F32)).astype(BF)
    return total + dot(high, pick_ref[:, at]) + dot(low, pick_ref[:, at])


def head_kernel(own_ref, recv_ref, a_hbm, extra_ref, pick_ref, inv_ref, inv_row_ref, label_ref, mask_ref,
                ws_ref, wn_ref, bias_ref,
                d_ref, own_grad_ref, out_ref, g_self_ref, g_neigh_ref, g_bias_ref, sums_ref,
                a_ref, table_ref, mean_ref, ws_pad, wn_pad, scaled_ref, sems):
    n_own = own_ref.shape[0]
    n_cls = ws_ref.shape[0]
    copies = load_adjacency(a_hbm, a_ref, sems)
    table_ref[:n_own] = own_ref[...]
    table_ref[n_own:] = recv_ref[...]
    picked = dot(pick_ref[...], table_ref[...]).astype(BF)
    ws_pad[...] = jnp.zeros_like(ws_pad)
    wn_pad[...] = jnp.zeros_like(wn_pad)
    ws_pad[:n_cls] = ws_ref[...].astype(F32)
    wn_pad[:n_cls] = wn_ref[...].astype(F32)
    w_self = ws_pad[...].astype(BF)
    w_neigh = wn_pad[...].astype(BF)
    sums_ref[...] = jnp.zeros_like(sums_ref)
    g_bias_ref[...] = jnp.zeros_like(g_bias_ref)
    for copy in copies:
        copy.wait()

    def one(t, _):
        mean = aggregate(a_ref, extra_ref, table_ref, picked, inv_ref, t)
        mean_ref[rows_at(t)] = mean
        at = rows_at(t)
        logits = dot_t(w_self, own_ref[at]) + dot_t(w_neigh, mean) + bias_ref[:, :1]
        cls = lax.broadcasted_iota(jnp.int32, (CLS, TILE), 0)
        logits = jnp.where(cls < n_cls, logits, -jnp.inf)
        shifted = logits - jnp.max(logits, axis=0, keepdims=True)
        exps = jnp.exp(shifted)
        total = jnp.sum(exps, axis=0, keepdims=True)
        is_label = cls == label_ref[:, at]
        picked_log = jnp.sum(jnp.where(is_label, shifted, 0.0), axis=0, keepdims=True) - jnp.log(total)
        mask = mask_ref[:, at]
        grad = (exps / total - jnp.where(is_label, 1.0, 0.0)) * mask
        for half in range(TILE // LANES):
            lanes = slice(half * LANES, (half + 1) * LANES)
            sums_ref[0:1] += -(mask * picked_log)[:, lanes]
            sums_ref[1:2] += mask[:, lanes]
            g_bias_ref[...] += grad[:, lanes]
        grad_bf = grad.astype(BF)
        d_ref[:, at] = grad_bf
        scaled_ref[:, at] = (grad_bf.astype(F32) * inv_row_ref[:, at]).astype(BF)
        return 0

    lax.fori_loop(0, n_own // TILE, one, 0)
    g_self_ref[...] = dot(d_ref[...], own_ref[...])
    g_neigh_ref[...] = dot(d_ref[...], mean_ref[...])

    def back(t, _):
        own_grad_ref[:, rows_at(t)] = column_product(scaled_ref[...], a_ref, extra_ref, pick_ref, t)
        return 0

    lax.fori_loop(0, n_own // TILE, back, 0)

    def back_recv(t, _):
        part = column_product(scaled_ref[...], a_ref, extra_ref, pick_ref, t + n_own // TILE)
        part = jnp.concatenate([part, jnp.zeros((LANES - CLS, TILE), F32)], axis=0)
        out_ref[rows_at(t)] = part.T.astype(BF)
        return 0

    lax.fori_loop(0, out_ref.shape[0] // TILE, back_recv, 0)


def middle_kernel(returned_ref, own_grad_ref, d_ref, own_ref, prev_ref, mean_ref, a_hbm, extra_ref, pick_ref, inv_row_ref,
                  send_row_ref, ws3_ref, wn3_ref, w_neigh_ref,
                  d_out_ref, own_out_ref, out_ref, g_self_ref, g_neigh_ref, g_bias_ref,
                  a_ref, scaled_ref, ws_pad, wn_pad, sems):
    n_own = own_ref.shape[0]
    width = own_ref.shape[1]
    n_cls = ws3_ref.shape[0]
    copies = load_adjacency(a_hbm, a_ref, sems)
    ws_pad[...] = jnp.zeros_like(ws_pad)
    wn_pad[...] = jnp.zeros_like(wn_pad)
    ws_pad[:n_cls] = ws3_ref[...].astype(F32)
    wn_pad[:n_cls] = wn3_ref[...].astype(F32)
    ws3 = ws_pad[...].T.astype(BF)
    wn3 = wn_pad[...].T.astype(BF)
    g_bias_ref[...] = jnp.zeros_like(g_bias_ref)
    eye = identity()

    def one(t, _):
        at = rows_at(t)
        sums = owner_sums(send_row_ref, returned_ref, t).T[:CLS]
        d_sum = (own_grad_ref[:, at] + sums).astype(BF)
        zero = jnp.zeros((LANES - CLS, TILE), F32)
        grown = jnp.concatenate([d_ref[:, at].astype(F32), zero], axis=0).astype(BF)
        d_sum = jnp.concatenate([d_sum.astype(F32), zero], axis=0).astype(BF)
        grad = dot(ws3, grown) + dot(wn3, d_sum)
        grad = jnp.where(dot_t(eye, own_ref[at]) > 0.0, grad, 0.0)
        for half in range(TILE // LANES):
            g_bias_ref[...] += grad[:, half * LANES:(half + 1) * LANES]
        d_out_ref[:, at] = grad.astype(BF)
        scaled_ref[:, at] = (dot(w_neigh_ref[...], grad.astype(BF)) * inv_row_ref[:, at]).astype(BF)
        return 0

    lax.fori_loop(0, n_own // TILE, one, 0)
    for copy in copies:
        copy.wait()

    def back_recv(t, _):
        part = column_product(scaled_ref[...], a_ref, extra_ref, pick_ref, t + n_own // TILE)
        out_ref[rows_at(t)] = part.T.astype(BF)
        return 0

    lax.fori_loop(0, out_ref.shape[0] // TILE, back_recv, 0)

    def back(t, _):
        own_out_ref[:, rows_at(t)] = column_product(scaled_ref[...], a_ref, extra_ref, pick_ref, t)
        return 0

    lax.fori_loop(0, n_own // TILE, back, 0)
    g_self_ref[...] = dot(d_out_ref[...], prev_ref[...]).T
    g_neigh_ref[...] = dot(d_out_ref[...], mean_ref[...]).T


def first_kernel(returned_ref, own_grad_ref, d_ref, own_ref, prev_ref, mean_ref, send_row_ref, w_self_ref,
                 g_self_ref, g_neigh_ref, g_bias_ref, d_out_ref):
    n_own = own_ref.shape[0]
    g_bias_ref[...] = jnp.zeros_like(g_bias_ref)
    eye = identity()

    def one(t, _):
        at = rows_at(t)
        sums = owner_sums(send_row_ref, returned_ref, t).T
        grad = dot(w_self_ref[...], d_ref[:, at]) + (own_grad_ref[:, at] + sums)
        grad = jnp.where(dot_t(eye, own_ref[at]) > 0.0, grad, 0.0)
        for half in range(TILE // LANES):
            g_bias_ref[...] += grad[:, half * LANES:(half + 1) * LANES]
        d_out_ref[:, at] = grad.astype(BF)
        return 0

    lax.fori_loop(0, n_own // TILE, one, 0)
    g_self_ref[...] = dot(d_out_ref[...], prev_ref[...]).T
    g_neigh_ref[...] = dot(d_out_ref[...], mean_ref[...]).T


def call(kernel, args, outs, scratch, name, flops, any_arg=None):
    return pl.pallas_call(
        kernel,
        in_specs=[ANY if i == any_arg else VMEM for i in range(len(args))],
        out_specs=[VMEM] * len(outs),
        out_shape=[jax.ShapeDtypeStruct(shape, dtype) for shape, dtype in outs],
        scratch_shapes=scratch,
        compiler_params=pltpu.CompilerParams(vmem_limit_bytes=VMEM_LIMIT),
        cost_estimate=pl.CostEstimate(flops=flops, bytes_accessed=16 * 2**20, transcendentals=0),
        name=name,
    )(*args)


def solution(mesh):
    parts = mesh.shape[AXIS]

    def device_step(features, labels, train_mask, send_idx, src_idx, dst_idx, inv_deg,
                    w_self_1, w_neigh_1, bias_1, w_self_2, w_neigh_2, bias_2,
                    w_self_3, w_neigh_3, bias_3):
        n_own, f_in = features.shape
        n_recv = send_idx.size
        rows = n_own + n_recv
        hid = w_self_2.shape[0]
        n_cls = w_self_3.shape[1]
        per_peer = send_idx.shape[1]
        dense = 2 * n_own * rows * hid

        def exchange(array):
            width = array.shape[1]
            moved = lax.all_to_all(array.reshape(parts, per_peer, width), AXIS, 0, 0, tiled=True)
            return moved.reshape(n_recv, width)

        send_flat = send_idx.reshape(-1)
        send_col = jnp.broadcast_to(send_flat[:, None], (n_recv, LANES))
        send_row = send_flat[None, :]
        inv_cols = jnp.broadcast_to(inv_deg[:, None], (n_own, LANES))
        inv_row = inv_deg[None, :]
        own_0 = jnp.pad(features, ((0, 0), (0, LANES - f_in)))
        w_self_1p = jnp.pad(w_self_1, ((0, LANES - f_in), (0, 0)))
        w_neigh_1p = jnp.pad(w_neigh_1, ((0, LANES - f_in), (0, 0)))
        bias_3c = jnp.broadcast_to(jnp.pad(bias_3, (0, CLS - n_cls))[:, None], (CLS, LANES))

        out_0, = call(gather_kernel, (own_0, send_col), [((n_recv, LANES), BF)], [], 'gather_features', dense // 8)
        recv_0 = exchange(out_0)
        adj, extra, pick = build_adjacency(dst_idx, src_idx, n_own, rows)

        def scratch(width):
            return [pltpu.VMEM((n_own, rows), BF), pltpu.VMEM((rows, width), BF)]

        sems = pltpu.SemaphoreType.DMA((8,))

        def layer(own, recv, w_self, w_neigh, bias, name):
            width = own.shape[1]
            return call(layer_kernel,
                        (own, recv, adj, extra, pick, inv_cols, send_col, w_self, w_neigh, bias[None, :]),
                        [((n_own, hid), BF), ((n_own, width), BF), ((n_recv, hid), BF)],
                        scratch(width) + [sems], name, dense, any_arg=2)

        hidden_1, mean_1, out_1 = layer(own_0, recv_0, w_self_1p, w_neigh_1p, bias_1, 'layer_1')
        recv_1 = exchange(out_1)
        hidden_2, mean_2, out_2 = layer(hidden_1, recv_1, w_self_2, w_neigh_2, bias_2, 'layer_2')
        recv_2 = exchange(out_2)
        d_3, own_grad_3, back_3, g_self_3, g_neigh_3, g_bias_3, sums = call(
            head_kernel,
            (hidden_2, recv_2, adj, extra, pick, inv_cols, inv_row, labels[None, :], train_mask[None, :],
             w_self_3.T, w_neigh_3.T, bias_3c),
            [((CLS, n_own), BF), ((CLS, n_own), F32), ((n_recv, LANES), BF), ((CLS, hid), F32), ((CLS, hid), F32),
             ((CLS, LANES), F32), ((8, LANES), F32)],
            scratch(hid) + [pltpu.VMEM((n_own, hid), BF), pltpu.VMEM((CLS, hid), F32), pltpu.VMEM((CLS, hid), F32),
                            pltpu.VMEM((CLS, n_own), BF), sems],
            'head', 2 * dense, any_arg=2)
        returned_3 = exchange(back_3)
        d_2, own_grad_2, back_2, g_self_2, g_neigh_2, g_bias_2 = call(
            middle_kernel,
            (returned_3, own_grad_3, d_3, hidden_2, hidden_1, mean_2, adj, extra, pick, inv_row, send_row,
             w_self_3.T, w_neigh_3.T, w_neigh_2),
            [((hid, n_own), BF), ((hid, n_own), F32), ((n_recv, hid), BF), ((hid, hid), F32), ((hid, hid), F32),
             ((hid, LANES), F32)],
            [pltpu.VMEM((n_own, rows), BF), pltpu.VMEM((hid, n_own), BF), pltpu.VMEM((LANES, hid), F32),
             pltpu.VMEM((LANES, hid), F32), sems],
            'middle', 2 * dense, any_arg=6)
        returned_2 = exchange(back_2)
        g_self_1, g_neigh_1, g_bias_1 = call(
            first_kernel,
            (returned_2, own_grad_2, d_2, hidden_1, own_0, mean_1, send_row, w_self_2),
            [((LANES, hid), F32), ((LANES, hid), F32), ((hid, LANES), F32)],
            [pltpu.VMEM((hid, n_own), BF)], 'first', dense)

        pieces = [g_self_1[:f_in], g_neigh_1[:f_in], g_self_2, g_neigh_2, g_self_3[:n_cls], g_neigh_3[:n_cls],
                  jnp.sum(g_bias_1, axis=1), jnp.sum(g_bias_2, axis=1), jnp.sum(g_bias_3, axis=1)[:n_cls],
                  jnp.sum(sums[:2], axis=1)]
        sizes = [piece.size for piece in pieces]
        slice_rows = -(-sum(sizes) // (parts * LANES))
        slice_rows = -(-slice_rows // 8) * 8
        flat = jnp.concatenate([piece.reshape(-1) for piece in pieces])
        flat = jnp.pad(flat, (0, parts * slice_rows * LANES - flat.shape[0])).reshape(parts, slice_rows, LANES)
        summed = jnp.sum(lax.all_to_all(flat, AXIS, 0, 0, tiled=True), axis=0)
        whole = lax.all_to_all(jnp.broadcast_to(summed[None], flat.shape), AXIS, 0, 0, tiled=True).reshape(-1)
        offsets = [sum(sizes[:i]) for i in range(len(sizes))]
        got = [whole[o:o + s].reshape(piece.shape) for o, s, piece in zip(offsets, sizes, pieces)]
        loss_sum, count = got[9][0], got[9][1]
        scale = 1.0 / count
        return (loss_sum / count,
                got[0] * scale, got[1] * scale, got[6] * scale,
                got[2] * scale, got[3] * scale, got[7] * scale,
                got[4].T * scale, got[5].T * scale, got[8] * scale)

    sharded = P(AXIS)
    whole = P()
    return jax.shard_map(device_step, mesh=mesh,
                         in_specs=(sharded,) * 7 + (whole,) * 9,
                         out_specs=(whole,) * 10, check_vma=False)
```

time: 1850 us -> 407 us (0.22)
  other arithmetic: 980 us -> 6.93 us
  waiting for transfers between devices: 645 us -> 72.9 us
  Pallas kernels: 0 us -> 135 us
  blocking collectives: 74.8 us -> 119 us
  matrix products: 28.9 us -> 0 us
    scatter-add x7 -> x0, other arithmetic: 961 us -> none  [the longest x3 545 us: aggregate(): jax.ops.segment_sum(gathered, dst_idx, num_segments=inv_deg.shape[0], ind...]
    psum x2 -> x0, waiting for transfers between devices: 525 us -> none  [device_step(): lax.psum((g_self_1, g_neigh_1, g_bias_1, g_self_2, g_neigh_2, g_bias_2, g...]
    pallas_call x0 -> x7, Pallas kernels: none -> 135 us  [the longest x6 117 us: call(): pl.pallas_call(kernel, in_specs=[ANY if i == any_arg else VMEM for i in r...]
    all_to_all x0 -> x3, blocking collectives: none -> 119 us  [the longest x1 45.8 us: exchange(): lax.all_to_all(array.reshape(parts, per_peer, width), AXIS, 0, 0, tiled=T...]
    psum x1 -> x0, blocking collectives: 74.8 us -> none  [device_step(): totals = lax.psum(jnp.stack([loss_sum, jnp.sum(train_mask)]), GROUP_AXIS)]
    all_to_all x5 -> x4, waiting for transfers between devices: 120 us -> 72.9 us  [exchange(): lax.all_to_all(array.reshape(parts, per_peer, width), AXIS, 0, 0, tiled=T...]
    dot_general x16 -> x0, matrix products: 28.9 us -> none  [the longest x3 6.68 us: layer(): jnp.dot(neigh_mean, w_neigh, preferred_element_type=jnp.float32)]
    gather x3 -> x0, local copies, waits for them, and re-layouts: 21.2 us -> none  [layer(): outgoing = jnp.take(hidden, send_flat, axis=0)]
  transfers between devices with their start and end apart: 7 -> 4, of which waited for: 7 -> 3; matrix products, arithmetic and copies ran while one was open for 1% -> 3% of each run, Pallas kernels for 0% -> 4%
where the time goes in v1:
time: 407 us
  Pallas kernels  135 us (33%)
  blocking collectives  119 us (29%)
  waiting for transfers between devices  72.9 us (18%)
  starting transfers between devices  38.2 us (9%)
  local copies, waits for them, and re-layouts  29.7 us (7%)
  other arithmetic  6.93 us (2%)
    pallas_call x6, Pallas kernels, call(): pl.pallas_call(kernel, in_specs=[ANY if i == any_arg else VMEM for i in r...  117 us
    all_to_all x4, waiting for transfers between devices, exchange(): lax.all_to_all(array.reshape(parts, per_peer, width), AXIS, 0, 0, tiled=T...  72.9 us
    all_to_all x1, blocking collectives, exchange(): lax.all_to_all(array.reshape(parts, per_peer, width), AXIS, 0, 0, tiled=T...  45.8 us
    all_to_all x4, starting transfers between devices, exchange(): lax.all_to_all(array.reshape(parts, per_peer, width), AXIS, 0, 0, tiled=T...  38.2 us
    all_to_all x1, blocking collectives, device_step(): lax.all_to_all(jnp.broadcast_to(summed[None], flat.shape), AXIS, 0, 0, ti...  36.8 us
    all_to_all x1, blocking collectives, device_step(): summed = jnp.sum(lax.all_to_all(flat, AXIS, 0, 0, tiled=True), axis=0)  36.8 us
    pallas_call x1, Pallas kernels, build_adjacency(): pl.pallas_call(build_kernel, grid_spec=pltpu.PrefetchScalarGridSpec(num_s...  18.2 us
    unnamed x24, local copies, waits for them, and re-layouts  12.7 us
  transfers between devices with their start and end apart: 4, of which 3 were waited for; matrix products, arithmetic and copies ran while one was open for 3% of the time, Pallas kernels for 4%

profile of v1, /device:TPU:1, one launch (start us, length us, event | category | flops | bytes accessed | tf_op | source)
XLA Modules:
  0.0 406.6 jit_solution(490964734416041113)
XLA Ops:
  0.6 0.8 copy.32
  1.5 0.1 broadcast_in_dim.20
  1.6 1.3 copy.31
  2.9 0.9 pad.26.own_ref.prev_ref
  3.8 1.3 broadcast_in_dim.21.send_col_ref
  5.2 5.6 %gather_features.1 = bf16[2048,128]{1,0:T(8,128)(2,1)} custom-call(bf16[2048,128]{1,0:T(8,128)(2,1)} %pad.26.own_ref.prev_ref, s32[2048,128]{1,0:T(8,128)} %broadcast_in_dim.21.send_col_ref), custom_call_target="tpu_custom_call" | custom-call | flops 536870912 | bytes 16777216 | tf_op jit(solution)/shard_map/gather_features/pallas_call | solution.py:384
  10.8 0.0 copy-start.8
  10.8 15.7 %all-to-all-start = ((bf16[256,8,128]{2,1,0:T(8,128)(2,1)}), bf16[256,8,128]{2,1,0:T(8,128)(2,1)S(1)}, u32[]{:S(2)}, u32[]{:S(2)}) async-start(bf16[256,8,128]{2,1,0:T(8,128)(2,1)} %bitcast.40), calls=%async_computation | async-start | bytes 1048576 | tf_op jit(solution)/shard_map/all_to_all | solution.py:412
  26.4 1.4 pad.29.w_self_ref
  27.9 1.4 pad.30.w_neigh_ref
  29.3 0.9 pad.28.src_ref
  30.2 0.9 pad.27.dst_ref
  31.1 1.9 convert_reduce_fusion.starts
  33.1 18.2 %build_adjacency.1 = (bf16[2048,4096]{1,0:T(8,128)(2,1)S(1)}, bf16[2048,128]{1,0:T(8,128)(2,1)S(1)}, bf16[128,4096]{1,0:T(8,128)(2,1)S(1)}) custom-call(s32[129]{0:T(256)S(1)} %convert_reduce_fusion.starts, s32[130,1,128]{2,1,0:T(1,128)S(1)} %pad.27.dst_ref, s32[130,1,128]{2,1,0:T(1,128)S(1)} %pad.28.src_ref), custom_call_target="tpu_custom_call" | custom-call | flops 4294967296 | bytes 16777216 | tf_op jit(solution)/shard_map/build_adjacency/pallas_call | solution.py:153
  51.3 0.0 copy-start
  51.3 5.7 %copy-done = bf16[2048,4096]{1,0:T(8,128)(2,1)} copy-done((bf16[2048,4096]{1,0:T(8,128)(2,1)}, bf16[2048,4096]{1,0:T(8,128)(2,1)S(1)}, u32[]{:S(2)}) %copy-start) | copy-done | bytes 16777240
  57.0 1.0 copy-done.1
  58.0 0.8 copy-done.2
  58.8 0.0 all-to-all-done
  58.8 0.0 copy-done.8
  58.8 1.3 broadcast_in_dim.44.inv_ref
  60.1 0.0 copy-done.3
  60.1 20.7 %layer_1.1 = (bf16[2048,256]{1,0:T(8,128)(2,1)}, bf16[2048,128]{1,0:T(8,128)(2,1)}, bf16[2048,256]{1,0:T(8,128)(2,1)}) custom-call(bf16[2048,128]{1,0:T(8,128)(2,1)} %pad.26.own_ref.prev_ref, bf16[2048,128]{1,0:T(8,128)(2,1)} %bitcast.39, bf16[2048,4096]{1,0:T(8,128)(2,1)} %copy-done, bf16[2048,128]{1,0:T(8,128)(2,1)} %copy-done.2, ...), custom_call_target="tpu_custom_call" | custom-call | flops 4294967296 | bytes 16777216 | tf_op jit(solution)/shard_map/layer_1/pallas_call | solution.py:384
  80.9 45.8 %all_to_all.35 = bf16[256,8,256]{2,1,0:T(8,128)(2,1)} all-to-all(bf16[256,8,256]{2,1,0:T(8,128)(2,1)} %bitcast.43), channel_id=1, replica_groups=mesh['gp'=256] {'gp'}, dimensions={0} | all-to-all | bytes 2097152 | tf_op jit(solution)/shard_map/all_to_all | solution.py:412
  126.6 21.4 %layer_2.1 = (bf16[2048,256]{1,0:T(8,128)(2,1)}, bf16[2048,256]{1,0:T(8,128)(2,1)}, bf16[2048,256]{1,0:T(8,128)(2,1)}) custom-call(bf16[2048,256]{1,0:T(8,128)(2,1)} %get-tuple-element.38.own_ref.prev_ref, bf16[2048,256]{1,0:T(8,128)(2,1)} %bitcast.38, bf16[2048,4096]{1,0:T(8,128)(2,1)} %copy-done, bf16[2048,128]{1,0:T(8,128)(2,1)} %copy-done.2, ...), custom_call_target="tpu_custom_call" | custom-call | flops 4294967296 | bytes 16777216 | tf_op jit(solution)/shard_map/layer_2/pallas_call | solution.py:384
  148.0 8.2 %all-to-all-start.2 = ((bf16[256,8,256]{2,1,0:T(8,128)(2,1)}), bf16[256,8,256]{2,1,0:T(8,128)(2,1)}, u32[]{:S(2)}, u32[]{:S(2)}) async-start(bf16[256,8,256]{2,1,0:T(8,128)(2,1)} %bitcast.42), calls=%async_computation.2 | async-start | bytes 2097152 | tf_op jit(solution)/shard_map/all_to_all | solution.py:412
  156.3 0.0 copy-done.9
  156.3 29.1 %all-to-all-done.2 = bf16[256,8,256]{2,1,0:T(8,128)(2,1)} async-done(((bf16[256,8,256]{2,1,0:T(8,128)(2,1)}), bf16[256,8,256]{2,1,0:T(8,128)(2,1)}, u32[]{:S(2)}, u32[]{:S(2)}) %all-to-all-start.2) | async-done | bytes 1048608 | tf_op jit(solution)/shard_map/all_to_all | solution.py:412
  185.4 0.7 broadcast_in_dim.50.bias_ref
  186.1 26.6 %head.1 = (bf16[48,2048]{1,0:T(8,128)(2,1)}, f32[48,2048]{1,0:T(8,128)}, bf16[2048,128]{1,0:T(8,128)(2,1)}, f32[48,256]{1,0:T(8,128)}, f32[48,256]{1,0:T(8,128)}, /*index=5*/f32[48,128]{1,0:T(8,128)}, f32[8,128]{1,0:T(8,128)}) custom-call(bf16[2048,256]{1,0:T(8,128)(2,1)} %get-tuple-element.40.own_ref, bf16[2048,256]{1,0:T(8,128)(2,1)} %bitcast.9.recv_ref, ...), custom_call_target="tpu_custom_call" | custom-call | flops 8589934592 | bytes 16777216 | tf_op jit(solution)/shard_map/head/pallas_call | solution.py:384
  212.7 6.7 %all-to-all-start.3 = ((bf16[256,8,128]{2,1,0:T(8,128)(2,1)}), bf16[256,8,128]{2,1,0:T(8,128)(2,1)S(1)}, u32[]{:S(2)}, u32[]{:S(2)}) async-start(bf16[256,8,128]{2,1,0:T(8,128)(2,1)} %bitcast.47), calls=%async_computation.3 | async-start | bytes 1048576 | tf_op jit(solution)/shard_map/all_to_all | solution.py:412
  219.4 0.7 broadcast_in_dim_reshape.4.send_row_ref
  220.1 18.7 %all-to-all-done.3 = bf16[256,8,128]{2,1,0:T(8,128)(2,1)S(1)} async-done(((bf16[256,8,128]{2,1,0:T(8,128)(2,1)}), bf16[256,8,128]{2,1,0:T(8,128)(2,1)S(1)}, u32[]{:S(2)}, u32[]{:S(2)}) %all-to-all-start.3) | async-done | bytes 524320 | tf_op jit(solution)/shard_map/all_to_all | solution.py:412
  238.8 0.8 copy-done.4
  239.6 34.1 %middle.1 = (bf16[256,2048]{1,0:T(8,128)(2,1)}, f32[256,2048]{1,0:T(8,128)}, bf16[2048,256]{1,0:T(8,128)(2,1)}, f32[256,256]{1,0:T(8,128)}, f32[256,256]{1,0:T(8,128)}, /*index=5*/f32[256,128]{1,0:T(8,128)}) custom-call(bf16[2048,128]{1,0:T(8,128)(2,1)} %bitcast.46, f32[48,2048]{1,0:T(8,128)} %get-tuple-element.43.own_grad_ref, ...), custom_call_target="tpu_custom_call" | custom-call | flops 8589934592 | bytes 16777216 | tf_op jit(solution)/shard_map/middle/pallas_call | solution.py:384
  273.7 7.6 %all-to-all-start.4 = ((bf16[256,8,256]{2,1,0:T(8,128)(2,1)}), bf16[256,8,256]{2,1,0:T(8,128)(2,1)}, u32[]{:S(2)}, u32[]{:S(2)}) async-start(bf16[256,8,256]{2,1,0:T(8,128)(2,1)} %bitcast.41), calls=%async_computation.4 | async-start | bytes 2097152 | tf_op jit(solution)/shard_map/all_to_all | solution.py:412
  281.4 0.0 copy-done.7
  281.4 0.1 reduce_sum.57
  281.5 0.0 copy-done.6
  281.5 0.0 copy-done.5
  281.5 0.8 slice_reduce_fusion
  282.3 1.0 reduce_sum.56
  283.3 1.1 copy.34
  284.4 1.1 copy.35
  285.5 25.0 %all-to-all-done.4 = bf16[256,8,256]{2,1,0:T(8,128)(2,1)} async-done(((bf16[256,8,256]{2,1,0:T(8,128)(2,1)}), bf16[256,8,256]{2,1,0:T(8,128)(2,1)}, u32[]{:S(2)}, u32[]{:S(2)}) %all-to-all-start.4) | async-done | bytes 1048608 | tf_op jit(solution)/shard_map/all_to_all | solution.py:412
  310.6 8.9 %first.1 = (f32[128,256]{1,0:T(8,128)}, f32[128,256]{1,0:T(8,128)}, f32[256,128]{1,0:T(8,128)}) custom-call(bf16[2048,256]{1,0:T(8,128)(2,1)} %bitcast.18.returned_ref, f32[256,2048]{1,0:T(8,128)} %get-tuple-element.47.own_grad_ref, bf16[256,2048]{1,0:T(8,128)(2,1)} %get-tuple-element.48.d_ref, bf16[2048,256]{1,0:T(8,128)(2,1)} %get-tuple-element.38.own_ref.prev_ref, ...), custom_call_target="tpu_custom_call" | custom-call | flops 4294967296 | bytes 16777216 | tf_op jit(solution)/shard_map/first/pallas_call | solution.py:384
  319.5 0.9 slice.62
  320.4 1.0 reduce_sum.55
  321.4 0.9 slice.63
  322.4 1.5 concatenate.3
  323.9 0.1 pad_bitcast_fusion
  323.9 36.8 %all_to_all.36 = f32[256,8,128]{2,1,0:T(8,128)S(1)} all-to-all(f32[256,8,128]{2,1,0:T(8,128)S(1)} %pad_bitcast_fusion), channel_id=1, replica_groups=mesh['gp'=256] {'gp'}, dimensions={0} | all-to-all | bytes 2097152 | tf_op jit(solution)/shard_map/all_to_all | solution.py:479
  360.7 0.3 reduce_sum.59
  361.0 0.1 broadcast_in_dim.51
  361.1 36.8 %all_to_all.37 = f32[256,8,128]{2,1,0:T(8,128)S(1)} all-to-all(f32[256,8,128]{2,1,0:T(8,128)S(1)} %broadcast_in_dim.51), channel_id=1, replica_groups=mesh['gp'=256] {'gp'}, dimensions={0} | all-to-all | bytes 2097152 | tf_op jit(solution)/shard_map/all_to_all | solution.py:480
  397.9 0.6 fusion.2
  399.1 0.5 slice_multiply_fusion.8
  399.6 0.6 slice_multiply_fusion.6
  401.6 0.7 mul.80
  402.3 0.7 mul.78
  402.9 0.3 slice.76
  403.2 0.6 fusion
  403.9 0.8 mul.87
  404.7 0.8 mul.85
  (16 shorter events, 0.1 us)
Async XLA Ops:
  10.8 48.0 %copy-start.8 = (f32[2048]{0:T(1024)S(1)}, f32[2048]{0:T(1024)}, u32[]{:S(2)}) copy-start(f32[2048]{0:T(1024)} %param.22) | copy-start | bytes 24580
  10.8 48.0 %all-to-all-start = ((bf16[256,8,128]{2,1,0:T(8,128)(2,1)}), bf16[256,8,128]{2,1,0:T(8,128)(2,1)S(1)}, u32[]{:S(2)}, u32[]{:S(2)}) async-start(bf16[256,8,128]{2,1,0:T(8,128)(2,1)} %bitcast.40), calls=%async_computation | async-start | bytes 1048576 | tf_op jit(solution)/shard_map/all_to_all | solution.py:412
  51.3 5.7 %copy-start = (bf16[2048,4096]{1,0:T(8,128)(2,1)}, bf16[2048,4096]{1,0:T(8,128)(2,1)S(1)}, u32[]{:S(2)}) copy-start(bf16[2048,4096]{1,0:T(8,128)(2,1)S(1)} %get-tuple-element.35.a_hbm) | copy-start | bytes 50331652
  57.0 1.0 copy-start.1
  58.0 0.8 copy-start.2
  58.8 1.3 copy-start.3
  126.6 29.6 %copy-start.9 = (f32[47]{0:T(128)S(1)}, f32[47]{0:T(128)}, u32[]{:S(2)}) copy-start(f32[47]{0:T(128)} %param.31) | copy-start | bytes 568
  148.0 37.4 %all-to-all-start.2 = ((bf16[256,8,256]{2,1,0:T(8,128)(2,1)}), bf16[256,8,256]{2,1,0:T(8,128)(2,1)}, u32[]{:S(2)}, u32[]{:S(2)}) async-start(bf16[256,8,256]{2,1,0:T(8,128)(2,1)} %bitcast.42), calls=%async_computation.2 | async-start | bytes 2097152 | tf_op jit(solution)/shard_map/all_to_all | solution.py:412
  212.7 26.1 %all-to-all-start.3 = ((bf16[256,8,128]{2,1,0:T(8,128)(2,1)}), bf16[256,8,128]{2,1,0:T(8,128)(2,1)S(1)}, u32[]{:S(2)}, u32[]{:S(2)}) async-start(bf16[256,8,128]{2,1,0:T(8,128)(2,1)} %bitcast.47), calls=%async_computation.3 | async-start | bytes 1048576 | tf_op jit(solution)/shard_map/all_to_all | solution.py:412
  238.8 0.8 copy-start.4
  239.6 41.8 %copy-start.7 = (f32[48,128]{1,0:T(8,128)S(1)}, f32[48,128]{1,0:T(8,128)}, u32[]{:S(2)}) copy-start(f32[48,128]{1,0:T(8,128)} %get-tuple-element.58) | copy-start | bytes 73732
  239.6 41.9 %copy-start.6 = (f32[48,256]{1,0:T(8,128)S(1)}, f32[48,256]{1,0:T(8,128)}, u32[]{:S(2)}) copy-start(f32[48,256]{1,0:T(8,128)} %get-tuple-element.54) | copy-start | bytes 147460
  239.6 41.9 %copy-start.5 = (f32[48,256]{1,0:T(8,128)S(1)}, f32[48,256]{1,0:T(8,128)}, u32[]{:S(2)}) copy-start(f32[48,256]{1,0:T(8,128)} %get-tuple-element.55) | copy-start | bytes 147460
  273.7 36.8 %all-to-all-start.4 = ((bf16[256,8,256]{2,1,0:T(8,128)(2,1)}), bf16[256,8,256]{2,1,0:T(8,128)(2,1)}, u32[]{:S(2)}, u32[]{:S(2)}) async-start(bf16[256,8,256]{2,1,0:T(8,128)(2,1)} %bitcast.41), calls=%async_computation.4 | async-start | bytes 2097152 | tf_op jit(solution)/shard_map/all_to_all | solution.py:412
